TPU v7x, 16 devices: a whole 2x2x2 slice. The times are simulated.
16 devices in a mesh: dp: 4 (over z, y), tp: 4 (over x, core).
Axes of the slice: x: 2, y: 2, z: 2, core: 2. Of those that a mesh axis runs over, the one named last changes fastest.
Arguments:
- x_in: bfloat16 [512, 1024], P('dp'), parts along dimension 0
- seq_lens: int32 [512], P('dp'), parts along dimension 0
- g_attn: bfloat16 [2, 1024], replicated
- g_mlp: bfloat16 [2, 1024], replicated
- w_q: bfloat16 [2, 1024, 2048], P(None, None, 'tp')
- b_q: bfloat16 [2, 2048], P(None, 'tp')
- w_k: bfloat16 [2, 1024, 1024], P(None, None, 'tp')
- b_k: bfloat16 [2, 1024], P(None, 'tp')
- w_v: bfloat16 [2, 1024, 1024], P(None, None, 'tp')
- b_v: bfloat16 [2, 1024], P(None, 'tp')
- w_o: bfloat16 [2, 2048, 1024], P(None, 'tp')
- w_gate: bfloat16 [2, 1024, 3072], P(None, None, 'tp')
- w_up: bfloat16 [2, 1024, 3072], P(None, None, 'tp')
- w_down: bfloat16 [2, 3072, 1024], P(None, 'tp')
- k_cache: bfloat16 [2, 512, 128, 8, 128], P(None, 'dp', None, 'tp'), parts along dimension 1
- v_cache: bfloat16 [2, 512, 128, 8, 128], P(None, 'dp', None, 'tp'), parts along dimension 1
Outputs:
- output 1: bfloat16 [512, 1024], P('dp'), parts along dimension 0
- output 2: bfloat16 [2, 512, 128, 8, 128], P(None, 'dp', None, 'tp'), parts along dimension 1
- output 3: bfloat16 [2, 512, 128, 8, 128], P(None, 'dp', None, 'tp'), parts along dimension 1
There are 4 independent parts. A program takes and returns all parts, laid end to end along the dimension named above; an argument that names none is the same for every part.
All inputs are finite; a program needn't handle non-finite values.
Results may differ from a plain program's by a relative error of at most 0.0187495.
Values are sent between devices in bfloat16 or wider.
A program may use at most 1 GiB of HBM per device.

v0:
```python
import jax
import jax.numpy as jnp
from jax import lax
from jax.sharding import PartitionSpec as P

ROPE_THETA = 1000000.0
EPS = 1e-6


def rms_norm(vec_in, gain_vec):
    vec_f32 = vec_in.astype(jnp.float32)
    mean_sq = jnp.mean(vec_f32 * vec_f32, axis=-1, keepdims=True)
    return (vec_f32 * lax.rsqrt(mean_sq + EPS) * gain_vec.astype(jnp.float32)).astype(jnp.bfloat16)


def rope_tables(seq_lens, head_dim):
    half_dim = head_dim // 2
    inv_freq = ROPE_THETA ** (-2.0 * jnp.arange(half_dim, dtype=jnp.float32) / head_dim)
    angles = seq_lens.astype(jnp.float32)[:, None] * inv_freq[None, :]
    angles = jnp.concatenate([angles, angles], axis=-1)[:, None, :]
    return jnp.cos(angles), jnp.sin(angles)


def apply_rope(vec_in, cos_tab, sin_tab):
    half_dim = vec_in.shape[-1] // 2
    rotated = jnp.concatenate([-vec_in[..., half_dim:], vec_in[..., :half_dim]], axis=-1)
    return vec_in * cos_tab + rotated * sin_tab


def attention(normed, seq_lens, cos_tab, sin_tab, w_q, b_q, w_k, b_k, w_v, b_v, k_cache, v_cache):
    num_rows, num_slots, kv_local, head_dim = k_cache.shape
    q_local = w_q.shape[1] // head_dim
    group_size = q_local // kv_local
    q_full = jnp.dot(normed, w_q, preferred_element_type=jnp.float32) + b_q.astype(jnp.float32)
    q_rot = apply_rope(q_full.reshape(num_rows, q_local, head_dim), cos_tab, sin_tab).astype(jnp.bfloat16)
    k_full = jnp.dot(normed, w_k, preferred_element_type=jnp.float32) + b_k.astype(jnp.float32)
    k_rot = apply_rope(k_full.reshape(num_rows, kv_local, head_dim), cos_tab, sin_tab).astype(jnp.bfloat16)
    v_full = jnp.dot(normed, w_v, preferred_element_type=jnp.float32) + b_v.astype(jnp.float32)
    v_new = v_full.astype(jnp.bfloat16).reshape(num_rows, kv_local, head_dim)
    slot_ids = lax.broadcasted_iota(jnp.int32, (1, num_slots), 1)
    is_new = (slot_ids == seq_lens[:, None])[:, :, None, None]
    k_next = jnp.where(is_new, k_rot[:, None], k_cache)
    v_next = jnp.where(is_new, v_new[:, None], v_cache)
    q_grouped = q_rot.reshape(num_rows, kv_local, group_size, head_dim)
    scores = jnp.einsum("bkgd,bskd->bkgs", q_grouped, k_next, preferred_element_type=jnp.float32) * (head_dim ** -0.5)
    visible = (slot_ids <= seq_lens[:, None])[:, None, None, :]
    scores = jnp.where(visible, scores, -1e30)
    attn_probs = jax.nn.softmax(scores, axis=-1).astype(jnp.bfloat16)
    attn_out = jnp.einsum("bkgs,bskd->bkgd", attn_probs, v_next, preferred_element_type=jnp.float32)
    return attn_out.astype(jnp.bfloat16).reshape(num_rows, q_local * head_dim), k_next, v_next


def mlp_partial(normed, w_gate, w_up, w_down):
    gate_proj = jnp.dot(normed, w_gate, preferred_element_type=jnp.float32)
    up_proj = jnp.dot(normed, w_up, preferred_element_type=jnp.float32)
    hidden_act = (jax.nn.silu(gate_proj) * up_proj).astype(jnp.bfloat16)
    return jnp.dot(hidden_act, w_down, preferred_element_type=jnp.float32)


def add_residual(x_cur, delta):
    return (x_cur.astype(jnp.float32) + delta.astype(jnp.float32)).astype(jnp.bfloat16)


def solution(mesh):
    weight_col = P(None, None, "tp")
    weight_row = P(None, "tp", None)
    bias_col = P(None, "tp")
    cache_spec = P(None, "dp", None, "tp", None)
    in_specs = (P("dp", None), P("dp"), P(None, None), P(None, None), weight_col, bias_col, weight_col, bias_col, weight_col, bias_col, weight_row, weight_col, weight_col, weight_row, cache_spec, cache_spec)
    out_specs = (P("dp", None), cache_spec, cache_spec)

    def local_step(x_in, seq_lens, g_attn, g_mlp, w_q, b_q, w_k, b_k, w_v, b_v, w_o, w_gate, w_up, w_down, k_cache, v_cache):
        cos_tab, sin_tab = rope_tables(seq_lens, k_cache.shape[-1])
        x_cur = x_in
        k_list = []
        v_list = []
        for layer_idx in range(w_q.shape[0]):
            normed = rms_norm(x_cur, g_attn[layer_idx])
            attn_out, k_next, v_next = attention(normed, seq_lens, cos_tab, sin_tab, w_q[layer_idx], b_q[layer_idx], w_k[layer_idx], b_k[layer_idx], w_v[layer_idx], b_v[layer_idx], k_cache[layer_idx], v_cache[layer_idx])
            k_list.append(k_next)
            v_list.append(v_next)
            attn_part = jnp.dot(attn_out, w_o[layer_idx], preferred_element_type=jnp.float32).astype(jnp.bfloat16)
            x_cur = add_residual(x_cur, lax.psum(attn_part, "tp"))
            mlp_part = mlp_partial(rms_norm(x_cur, g_mlp[layer_idx]), w_gate[layer_idx], w_up[layer_idx], w_down[layer_idx]).astype(jnp.bfloat16)
            x_cur = add_residual(x_cur, lax.psum(mlp_part, "tp"))
        return x_cur, jnp.stack(k_list), jnp.stack(v_list)

    return jax.shard_map(local_step, mesh=mesh, in_specs=in_specs, out_specs=out_specs, check_vma=False)
```

profile of v0, /device:TPU:0, one launch (start us, length us, event | category | flops | bytes accessed | tf_op | source)
XLA Modules:
  0.0 285.2 jit_solution(14544077373774223934)
XLA Ops:
  7.2 0.7 convert_element_type.135
  7.9 0.7 iota_compare_fusion.1
  8.6 1.1 fusion.82
  9.7 0.8 slice_convert_fusion.4
  10.5 0.8 slice_convert_fusion.3
  11.3 1.7 convolution_add_fusion.1
  12.9 0.1 reshape.213
  13.0 0.2 reshape.212
  13.2 0.8 slice_convert_fusion.7
  14.0 0.8 slice_convert_fusion.6
  14.7 1.4 fusion.66
  16.2 0.1 broadcast_multiply_fusion
  16.3 0.3 fusion.141
  16.6 1.4 convolution_add_fusion.5
  18.1 0.2 slice_negate_fusion.1
  18.3 0.2 slice_negate_fusion.3
  18.5 0.2 fusion.125
  18.7 25.9 %broadcast_select_fusion.7 = (bf16[128,128,2,128]{3,2,1,0:T(2,128)(2,1)}, bf16[128,128,2,128]{3,2,1,0:T(2,128)(2,1)}) fusion(pred[128,128]{1,0:T(8,128)(4,1)S(1)} %get-tuple-element.38, bf16[2,128,128,2,128]{4,3,2,1,0:T(2,128)(2,1)} %param.30, bf16[128,2,128]{2,1,0:T(2,128)(2,1)S(1)} %fusion.125, bf16[2,128,128,2,128]{4,3,2,1,0:T(2,128)(2,1)} %param.31, ...), kind=kLoop, calls=%fused_computation.11 | loop fusion | flops 8388608 | bytes 33701888 | tf_op jit(solution)/shard_map/jit(_where)/select_n | solution.py:42
  44.6 8.1 %fusion.151 = (f32[128,2,2]{2,1,0:T(2,128)S(1)}, f32[128,2,2,128]{3,2,1,0:T(2,128)S(1)}) fusion(bf16[128,128,2,128]{3,2,1,0:T(2,128)(2,1)} %get-tuple-element.25, pred[128,128]{1,0:T(8,128)(4,1)S(1)} %get-tuple-element.37, f32[128,2,2,64]{3,2,1,0:T(2,128)S(1)} %bitcast.88, f32[128,2,2,64]{3,2,1,0:T(2,128)S(1)} %bitcast.87, ...), kind=kOutput, calls=%fused_computation.169 | convolution fusion | flops 17367168 | bytes 9324544 | tf_op jit(solution)/shard_map/sub | solution.py:48
  52.7 5.8 %fusion.54 = bf16[128,2,2,128]{3,2,1,0:T(2,128)(2,1)S(1)} fusion(bf16[128,128,2,128]{3,2,1,0:T(2,128)(2,1)} %get-tuple-element.26, f32[128,2,2,128]{3,2,1,0:T(2,128)S(1)} %get-tuple-element.40, f32[128,2,2]{2,1,0:T(2,128)S(1)} %get-tuple-element.39), kind=kOutput, calls=%fused_computation.52 | convolution fusion | flops 16973824 | bytes 8783872 | tf_op jit(solution)/shard_map/bkgs,bskd->bkgd/dot_general | solution.py:49
  58.6 2.3 convolution_convert_fusion.1
  61.0 31.3 %all-reduce.5.cloned.1.call-done = bf16[128,1024]{1,0:T(8,128)(2,1)} async-done(((bf16[128,1024]{1,0:T(8,128)(2,1)}), bf16[128,1024]{1,0:T(8,128)(2,1)}) %all-reduce.5.cloned.1.call-update) | async-done | bytes 262160 | tf_op jit(solution)/shard_map/psum | solution.py:83
  92.3 1.1 fusion.86
  93.4 1.8 fusion.20
  95.3 3.5 %fusion.30 = bf16[128,1024]{1,0:T(8,128)(2,1)} fusion(bf16[2,768,1024]{2,1,0:T(8,128)(2,1)} %param.29, bf16[2,1024,768]{2,1,0:T(8,128)(2,1)} %param.28, f32[128,768]{1,0:T(8,128)S(1)} %fusion.20, bf16[128,1024]{1,0:T(8,128)(2,1)S(1)} %get-tuple-element.6, f32[1024]{0:T(1024)S(1)} %bitcast.96, f32[128]{0:T(128)S(1)} %add_rsqrt_fusion.2), kind=kOutput, calls=%fused_computation.40 | convolution fusion | flops 403898368 | bytes 4067840 | tf_op jit(solution)/shard_map/dot_general | solution.py:57
  98.7 0.2 all-reduce.9.cloned.1.call-start
  99.0 28.3 %all-reduce.7.cloned.1.call-done = bf16[128,1024]{1,0:T(8,128)(2,1)} async-done(((bf16[128,1024]{1,0:T(8,128)(2,1)}), bf16[128,1024]{1,0:T(8,128)(2,1)}) %all-reduce.7.cloned.1.call-update) | async-done | bytes 262160 | tf_op jit(solution)/shard_map/psum | solution.py:85
  127.3 1.1 fusion.90
  128.4 1.1 fusion.92
  129.5 1.5 convolution_add_fusion
  131.1 0.1 reshape.217
  131.2 0.2 reshape.216
  131.3 0.2 fusion.67
  131.6 1.3 convolution_add_fusion.3
  133.0 0.2 slice_negate_fusion
  133.2 0.2 slice_negate_fusion.2
  133.4 0.2 fusion.127
  133.6 25.9 %broadcast_select_fusion.5 = (bf16[128,128,2,128]{3,2,1,0:T(2,128)(2,1)}, bf16[128,128,2,128]{3,2,1,0:T(2,128)(2,1)}) fusion(pred[128,128]{1,0:T(8,128)(4,1)S(1)} %get-tuple-element.38, bf16[2,128,128,2,128]{4,3,2,1,0:T(2,128)(2,1)} %param.30, bf16[128,2,128]{2,1,0:T(2,128)(2,1)S(1)} %fusion.127, bf16[2,128,128,2,128]{4,3,2,1,0:T(2,128)(2,1)} %param.31, ...), kind=kLoop, calls=%fused_computation.9 | loop fusion | flops 8388608 | bytes 33701888 | tf_op jit(solution)/shard_map/jit(_where)/select_n | solution.py:42
  159.6 8.1 %fusion.152 = (f32[128,2,2]{2,1,0:T(2,128)S(1)}, f32[128,2,2,128]{3,2,1,0:T(2,128)S(1)}) fusion(bf16[128,128,2,128]{3,2,1,0:T(2,128)(2,1)} %get-tuple-element.23, pred[128,128]{1,0:T(8,128)(4,1)S(1)} %get-tuple-element.37, f32[128,2,2,64]{3,2,1,0:T(2,128)S(1)} %bitcast.86, f32[128,2,2,64]{3,2,1,0:T(2,128)S(1)} %bitcast.85, ...), kind=kOutput, calls=%fused_computation.170 | convolution fusion | flops 17367168 | bytes 9324544 | tf_op jit(solution)/shard_map/sub | solution.py:48
  167.7 5.7 %fusion.57 = bf16[128,2,2,128]{3,2,1,0:T(2,128)(2,1)S(1)} fusion(bf16[128,128,2,128]{3,2,1,0:T(2,128)(2,1)} %get-tuple-element.24, f32[128,2,2,128]{3,2,1,0:T(2,128)S(1)} %get-tuple-element.42, f32[128,2,2]{2,1,0:T(2,128)S(1)} %get-tuple-element.41), kind=kOutput, calls=%fused_computation.53 | convolution fusion | flops 16973824 | bytes 8783872 | tf_op jit(solution)/shard_map/bkgs,bskd->bkgd/dot_general | solution.py:49
  173.5 2.2 convolution_convert_fusion
  175.7 0.3 all-reduce.11.cloned.1.call-start
  176.0 41.5 %broadcast_select_fusion.1 = (bf16[1,128,128,2,128]{4,3,2,1,0:T(2,128)(2,1)}, bf16[1,128,128,2,128]{4,3,2,1,0:T(2,128)(2,1)}, bf16[1,128,128,2,128]{4,3,2,1,0:T(2,128)(2,1)}, bf16[1,128,128,2,128]{4,3,2,1,0:T(2,128)(2,1)}) fusion(pred[128,128]{1,0:T(8,128)(4,1)S(1)} %get-tuple-element.38, bf16[2,128,128,2,128]{4,3,2,1,0:T(2,128)(2,1)} %param.31, ...), kind=kLoop, calls=%fused_computation.5 | loop fusion | flops 16777216 | bytes 67387392 | tf_op jit(solution)/shard_map/jit(_where)/select_n | solution.py:43
  217.6 1.2 fusion.94
  218.7 1.8 fusion.14
  220.6 3.5 %fusion.33 = bf16[128,1024]{1,0:T(8,128)(2,1)} fusion(bf16[2,768,1024]{2,1,0:T(8,128)(2,1)} %param.29, bf16[2,1024,768]{2,1,0:T(8,128)(2,1)} %param.28, f32[128,768]{1,0:T(8,128)S(1)} %fusion.14, bf16[128,1024]{1,0:T(8,128)(2,1)S(1)} %get-tuple-element.4, f32[1024]{0:T(1024)S(1)} %bitcast.91, f32[128]{0:T(128)S(1)} %add_rsqrt_fusion), kind=kOutput, calls=%fused_computation.41 | convolution fusion | flops 403898368 | bytes 4067840 | tf_op jit(solution)/shard_map/dot_general | solution.py:57
  224.0 52.9 %pad_maximum_fusion = (bf16[2,128,128,2,128]{4,3,2,1,0:T(2,128)(2,1)}, bf16[2,128,128,2,128]{4,3,2,1,0:T(2,128)(2,1)}) fusion(bf16[1,128,128,2,128]{4,3,2,1,0:T(2,128)(2,1)} %get-tuple-element.21, bf16[1,128,128,2,128]{4,3,2,1,0:T(2,128)(2,1)} %get-tuple-element.22, bf16[1,128,128,2,128]{4,3,2,1,0:T(2,128)(2,1)} %get-tuple-element.8, ...), kind=kLoop, calls=%fused_computation.2 | loop fusion | flops 16777216 | bytes 67108864 | tf_op jit(solution)/shard_map/stack | solution.py:86
  276.9 1.7 fusion.97
  (28 shorter events, 0.6 us)
Async XLA Ops:
  7.2 85.1 %all-reduce.5.cloned.1.call-start = ((), (), s32[]{:S(2)}) async-start(), calls=%async_computation | async-start | bytes 524288 | tf_op jit(solution)/shard_map/psum | solution.py:83
  52.7 8.2 %copy-start.2 = (bf16[2,1024]{1,0:T(2,128)(2,1)S(1)}, bf16[2,1024]{1,0:T(2,128)(2,1)}, u32[]{:S(2)}) copy-start(bf16[2,1024]{1,0:T(2,128)(2,1)} %param.19) | copy-start | bytes 12292
  52.7 39.6 %copy-start.1 = (bf16[128,1024]{1,0:T(8,128)(2,1)S(1)}, bf16[128,1024]{1,0:T(8,128)(2,1)}, u32[]{:S(2)}) copy-start(bf16[128,1024]{1,0:T(8,128)(2,1)} %param.16) | copy-start | bytes 786436
  58.5 72.9 %copy-start.3 = (bf16[2,1024,256]{2,1,0:T(8,128)(2,1)S(1)}, bf16[2,1024,256]{2,1,0:T(8,128)(2,1)}, u32[]{:S(2)}) copy-start(bf16[2,1024,256]{2,1,0:T(8,128)(2,1)} %param.24) | copy-start | bytes 3145732
  60.9 66.4 %all-reduce.7.cloned.1.call-start = ((), (), s32[]{:S(2)}) async-start(), calls=%async_computation.1 | async-start | bytes 524288 | tf_op jit(solution)/shard_map/psum | solution.py:85
  98.7 118.8 %all-reduce.9.cloned.1.call-start = ((), (), s32[]{:S(2)}) async-start(), calls=%async_computation.2 | async-start | bytes 524288 | tf_op jit(solution)/shard_map/psum | solution.py:83
  175.7 41.8 %copy-start = (bf16[128,1024]{1,0:T(8,128)(2,1)S(1)}, bf16[128,1024]{1,0:T(8,128)(2,1)}, u32[]{:S(2)}) copy-start(bf16[128,1024]{1,0:T(8,128)(2,1)} %all-reduce.7.cloned.1.call-done) | copy-start | bytes 786436
  175.7 101.2 %all-reduce.11.cloned.1.call-start = ((), (), s32[]{:S(2)}) async-start(), calls=%async_computation.3 | async-start | bytes 524288 | tf_op jit(solution)/shard_map/psum | solution.py:85
Sparse Core Ops, SparseCore 0:
  61.0 31.2 all-reduce.4
  98.9 28.4 all-reduce.6
  175.9 28.4 all-reduce.8
  224.2 28.4 all-reduce.10
where the time goes:
time: 286 us; the launch traced here: 285 us
  other arithmetic  160 us (56%)
  waiting for transfers between devices  59.8 us (21%)
  matrix products  50.3 us (18%)
  between operations  14.1 us (5%)
    another operation x1, other arithmetic, local_step(): return (x_cur, jnp.stack(k_list), jnp.stack(v_list))  52.9 us
    select_n x2, other arithmetic, attention(): k_next = jnp.where(is_new, k_rot[:, None], k_cache)  51.8 us
    select_n x1, other arithmetic, attention(): v_next = jnp.where(is_new, v_new[:, None], v_cache)  41.5 us
    psum x2, waiting for transfers between devices, local_step(): x_cur = add_residual(x_cur, lax.psum(attn_part, 'tp'))  31.3 us
    psum x2, waiting for transfers between devices, local_step(): x_cur = add_residual(x_cur, lax.psum(mlp_part, 'tp'))  28.4 us
    sub x2, matrix products, attention(): attn_probs = jax.nn.softmax(scores, axis=-1).astype(jnp.bfloat16)  16.2 us
    dot_general x2, matrix products, attention(): jnp.einsum('bkgs,bskd->bkgd', attn_probs, v_next, preferred_element_type=...  11.5 us
    dot_general x2, matrix products, mlp_partial(): return jnp.dot(hidden_act, w_down, preferred_element_type=jnp.float32)  6.91 us
  transfers between devices with their start and end apart: 4, of which 2 were waited for; matrix products, arithmetic and copies ran while one was open for 33% of the time, Pallas kernels for 0%

commit v1 on v0

v1 whole, which is shorter than its diff:
```python
import functools

import jax
import jax.numpy as jnp
import numpy as np
from jax import lax
from jax.experimental import pallas as pl
from jax.experimental.pallas import tpu as pltpu
from jax.sharding import PartitionSpec as P

ROPE_THETA = 1000000.0
EPS = 1e-6
F32 = jnp.float32
BF16 = jnp.bfloat16
MESH = pl.DeviceIdType.MESH
BLK = 8


def dot(lhs, rhs):
    return jnp.dot(lhs, rhs, preferred_element_type=F32)


def dot_nt(lhs, rhs):
    return lax.dot_general(lhs, rhs, (((1,), (1,)), ((), ())), preferred_element_type=F32)


def one_hot(shape, hit):
    rows = lax.broadcasted_iota(jnp.int32, shape, 0)
    cols = lax.broadcasted_iota(jnp.int32, shape, 1)
    return jnp.where(hit(rows, cols), 1.0, 0.0).astype(BF16)


def step_kernel(chunk, x_ref, lens_ref, freq_ref, g_attn_ref, g_mlp_ref, bq_ref, bk_ref, bv_ref,
                wq_hbm, wk_hbm, wv_hbm, wo_hbm, wg_hbm, wu_hbm, wd_hbm, kc_hbm, vc_hbm,
                xo_ref, ko_ref, vo_ref,
                wq, wk, wv, wo, wg, wu, wd,
                spread, gather, ungather, kpat, vpat, qlhs, scores, rows_out, limit, ppat, cos_t, sin_t,
                part, recv_a, mid, recv_b, xs,
                w_sem, k_sem, v_sem, send_sem, recv_sem):
    layers, batch, slots2, head = ko_ref.shape
    heads = wq.shape[2] // head
    kv = wk.shape[2] // head
    group = heads // kv
    n_chunks = batch // chunk
    half = chunk // 2
    blocks = chunk // BLK
    tp = lax.axis_index("tp")
    core = lax.rem(tp, 2)
    chip = tp // 2
    core_peer = {"tp": chip * 2 + (1 - core)}
    chip_peer = {"tp": (1 - chip) * 2 + core}

    weights = ((wq_hbm, wq), (wk_hbm, wk), (wv_hbm, wv), (wo_hbm, wo), (wg_hbm, wg), (wu_hbm, wu), (wd_hbm, wd))

    def weight_copy(layer, idx):
        src, dst = weights[idx]
        return pltpu.make_async_copy(src.at[layer], dst.at[layer], w_sem.at[layer, idx])

    def cache_copy(src, dst, sem, layer, blk):
        return pltpu.make_async_copy(src.at[layer, pl.ds(blk * BLK, BLK)], dst.at[layer, pl.ds(blk * BLK, BLK)], sem.at[layer, blk])

    def start_weights(layer, idxs):
        for idx in idxs:
            weight_copy(layer, idx).start()

    def wait_weights(layer, idxs):
        for idx in idxs:
            weight_copy(layer, idx).wait()

    def start_cache(layer, c):
        for src, dst, sem in ((kc_hbm, ko_ref, k_sem), (vc_hbm, vo_ref, v_sem)):
            @pl.loop(0, blocks)
            def _(i):
                cache_copy(src, dst, sem, layer, c * blocks + i).start()

    start_weights(0, (0, 1, 2))
    start_cache(0, 0)

    barrier = pltpu.get_barrier_semaphore()
    for peer in (core_peer, chip_peer):
        pl.semaphore_signal(barrier, inc=1, device_id=peer, device_id_type=MESH)
    pl.semaphore_wait(barrier, 2)

    spread[...] = one_hot(spread.shape, lambda r, c: c == (r % kv) * chunk + r // 16)
    gather[...] = one_hot(gather.shape, lambda r, c: c == (r % heads) * chunk + r // heads)
    ungather[...] = one_hot(ungather.shape, lambda r, c: r == (c % heads) * chunk + c // heads)
    lens = lens_ref[...].astype(F32)
    sq = (batch, batch)
    diag = lax.broadcasted_iota(jnp.int32, sq, 0) == lax.broadcasted_iota(jnp.int32, sq, 1)
    len_col = jnp.sum(jnp.where(diag, jnp.broadcast_to(lens, sq), 0.0), axis=1, keepdims=True)
    len_cols = jnp.broadcast_to(len_col, (batch, head))
    angles = len_cols * freq_ref[...]
    cos_t[...] = jnp.cos(angles)
    lane = lax.broadcasted_iota(jnp.int32, (batch, head), 1)
    sine = jnp.sin(angles)
    sin_t[...] = jnp.where(lane < head // 2, -sine, sine)
    len_bf = len_cols.astype(BF16)
    ppat[...] = dot(one_hot((batch * 16, batch), lambda r, c: c == r // 16), len_bf).astype(BF16)
    row_len = dot(one_hot((batch * heads, batch), lambda r, c: c == r // heads), len_bf)
    row_len = jnp.concatenate([row_len] * (slots2 // head), axis=1)
    lim_shape = (batch * heads, slots2)
    q_head = lax.broadcasted_iota(jnp.int32, lim_shape, 0) % heads
    own = lax.broadcasted_iota(jnp.int32, lim_shape, 1) % kv == q_head // group
    limit[...] = jnp.where(own, row_len, -1.0)
    slot_of = (lax.broadcasted_iota(jnp.int32, (16, head), 0) // kv).astype(F32).astype(BF16)

    def rms_norm(x_bf, gain_ref, layer):
        x = x_bf.astype(F32)
        mean_sq = jnp.mean(x * x, axis=-1, keepdims=True)
        return (x * lax.rsqrt(mean_sq + EPS) * gain_ref[pl.ds(layer, 1), :].astype(F32)).astype(BF16)

    def read_x(stage, c):
        src = x_ref if stage == 0 else xs.at[stage - 1]
        return src[pl.ds(c * chunk, chunk), :]

    def qkv(layer, c):
        h = rms_norm(read_x(2 * layer, c), g_attn_ref, layer)
        cos = cos_t[pl.ds(c * chunk, chunk), :]
        sin = sin_t[pl.ds(c * chunk, chunk), :]

        def rope(vec):
            return (vec * cos + pltpu.roll(vec, head // 2, 1) * sin).astype(BF16)

        def split(mat, n):
            return [mat[:, i * head:(i + 1) * head] for i in range(n)]

        q = dot(h, wq[layer]) + bq_ref[pl.ds(layer, 1), :].astype(F32)
        k = dot(h, wk[layer]) + bk_ref[pl.ds(layer, 1), :].astype(F32)
        v = dot(h, wv[layer]) + bv_ref[pl.ds(layer, 1), :].astype(F32)
        q_stack = jnp.concatenate([rope(m) for m in split(q, heads)], axis=0)
        k_stack = jnp.concatenate([rope(m) for m in split(k, kv)], axis=0)
        v_stack = jnp.concatenate([m.astype(BF16) for m in split(v, kv)], axis=0)
        kpat[...] = dot(spread[...], k_stack).astype(BF16)
        vpat[...] = dot(spread[...], v_stack).astype(BF16)
        q_rows = dot(gather[...], q_stack)
        first = lax.broadcasted_iota(jnp.int32, q_rows.shape, 0) % (2 * heads) < heads
        qlhs[...] = jnp.concatenate([jnp.where(first, q_rows, 0.0), jnp.where(first, 0.0, q_rows)], axis=1)

    def update(out_ref, pat_ref, layer, c, b):
        row = c * chunk + b
        old = out_ref[layer, row]
        pat = pat_ref[pl.ds(pl.multiple_of(b * 16, 16), 16), :]
        p = ppat[pl.ds(pl.multiple_of(row * 16, 16), 16), :]
        tiles = []
        for t in range(slots2 // 16):
            here = slot_of == p - jnp.asarray(t * (16 // kv), BF16)
            tiles.append(jnp.where(here, pat, old[t * 16:(t + 1) * 16, :]))
        new = jnp.concatenate(tiles, axis=0)
        out_ref[layer, row] = new
        return new

    def attn_scores(layer, c):
        @pl.loop(0, blocks)
        def _(i):
            cache_copy(kc_hbm, ko_ref, k_sem, layer, c * blocks + i).wait()
            for pair in range(BLK // 2):
                b = i * BLK + 2 * pair
                rhs = jnp.concatenate([update(ko_ref, kpat, layer, c, b), update(ko_ref, kpat, layer, c, b + 1)], axis=1)
                rows = pl.ds(pl.multiple_of(b * heads, 2 * heads), 2 * heads)
                scores[rows, :] = dot_nt(qlhs[rows, :].astype(BF16), rhs)

    def attn_softmax(c):
        s = scores[...] * (head ** -0.5)
        slot = (lax.broadcasted_iota(jnp.int32, s.shape, 1) // kv).astype(F32)
        s = jnp.where(slot <= limit[pl.ds(c * chunk * heads, chunk * heads), :], s, -1e30)
        e = jnp.exp(s - jnp.max(s, axis=-1, keepdims=True))
        scores[...] = e / jnp.sum(e, axis=-1, keepdims=True)

    def attn_values(layer, c):
        @pl.loop(0, blocks)
        def _(i):
            cache_copy(vc_hbm, vo_ref, v_sem, layer, c * blocks + i).wait()
            for pair in range(BLK // 2):
                b = i * BLK + 2 * pair
                rhs = jnp.concatenate([update(vo_ref, vpat, layer, c, b), update(vo_ref, vpat, layer, c, b + 1)], axis=1)
                rows = pl.ds(pl.multiple_of(b * heads, 2 * heads), 2 * heads)
                out = dot(scores[rows, :].astype(BF16), rhs)
                first = lax.broadcasted_iota(jnp.int32, (2 * heads, head), 0) < heads
                rows_out[rows, :] = jnp.where(first, out[:, :head], out[:, head:])

    def attn_project(layer, c):
        stacked = dot(ungather[...], rows_out[...].astype(BF16)).astype(BF16)
        attn = jnp.concatenate([stacked[i * chunk:(i + 1) * chunk, :] for i in range(heads)], axis=1)
        part[2 * layer * n_chunks + c] = dot(attn, wo[layer]).astype(BF16)

    def mlp(layer, c):
        h = rms_norm(read_x(2 * layer + 1, c), g_mlp_ref, layer)
        act = (jax.nn.silu(dot(h, wg[layer])) * dot(h, wu[layer])).astype(BF16)
        part[(2 * layer + 1) * n_chunks + c] = dot(act, wd[layer]).astype(BF16)

    mine = pl.ds(pl.multiple_of(core * half, half), half)
    other = pl.ds(pl.multiple_of((1 - core) * half, half), half)

    def send(hop, inst, src, dst, peer):
        return pltpu.make_async_remote_copy(src_ref=src, dst_ref=dst, send_sem=send_sem.at[hop, inst], recv_sem=recv_sem.at[hop, inst],
                                            device_id=peer, device_id_type=MESH)

    def hop_a(s, c):
        inst = s * n_chunks + c
        return send(0, inst, part.at[inst, other], recv_a.at[inst], core_peer)

    def hop_b(s, c):
        inst = s * n_chunks + c
        return send(1, inst, mid.at[inst], recv_b.at[inst], chip_peer)

    def hop_c(s, c):
        rows = pl.ds(pl.multiple_of(c * chunk + core * half, half), half)
        return send(2, s * n_chunks + c, xs.at[s, rows], xs.at[s, rows], core_peer)

    def sum_start(s, c):
        hop_a(s, c).start()

    def sum_cross(s, c):
        inst = s * n_chunks + c
        hop_a(s, c).wait_recv()
        mid[inst] = (part[inst, mine, :].astype(F32) + recv_a[inst].astype(F32)).astype(BF16)
        hop_b(s, c).start()

    def sum_share(s, c):
        inst = s * n_chunks + c
        hop_b(s, c).wait_recv()
        rows = pl.ds(pl.multiple_of(c * chunk + core * half, half), half)
        before = (x_ref if s == 0 else xs.at[s - 1])[rows, :]
        total = mid[inst].astype(F32) + recv_b[inst].astype(F32)
        xs[s, rows, :] = (before.astype(F32) + total).astype(BF16)
        hop_c(s, c).start()

    def sum_end(s, c):
        hop_c(s, c).wait_recv()

    def attention(layer, c, between=None):
        qkv(layer, c)
        attn_scores(layer, c)
        if between is not None:
            between()
        attn_softmax(c)
        attn_values(layer, c)
        attn_project(layer, c)
        sum_start(2 * layer, c)

    for layer in range(layers):
        s = 2 * layer
        if layer == 0:
            wait_weights(0, (0, 1, 2))
            start_weights(0, (3,))
            start_cache(0, 1)
            qkv(0, 0)
        else:
            wait_weights(layer, (0, 1, 2))
            sum_end(s - 1, 0)
            qkv(layer, 0)
        attn_scores(layer, 0)
        if layer > 0:
            sum_share(s - 1, 1)
        attn_softmax(0)
        attn_values(layer, 0)
        wait_weights(layer, (3,))
        attn_project(layer, 0)
        sum_start(s, 0)
        if layer == 0:
            start_weights(0, (4, 5, 6))
            start_weights(1, (0, 1, 2))
            start_cache(1, 0)
        else:
            sum_end(s - 1, 1)
        qkv(layer, 1)
        sum_cross(s, 0)
        attn_scores(layer, 1)
        attn_softmax(1)
        attn_values(layer, 1)
        attn_project(layer, 1)
        sum_start(s, 1)
        if layer == 0:
            start_cache(1, 1)
            start_weights(1, (3, 4, 5, 6))
        sum_share(s, 0)
        sum_cross(s, 1)
        wait_weights(layer, (4, 5, 6))
        sum_end(s, 0)
        mlp(layer, 0)
        sum_start(s + 1, 0)
        sum_share(s, 1)
        sum_cross(s + 1, 0)
        sum_end(s, 1)
        mlp(layer, 1)
        sum_start(s + 1, 1)
        sum_cross(s + 1, 1)
        sum_share(s + 1, 0)
        if layer == layers - 1:
            sum_end(s + 1, 0)
            sum_share(s + 1, 1)
            sum_end(s + 1, 1)

    for s in range(2 * layers):
        for c in range(n_chunks):
            hop_a(s, c).wait_send()
            hop_b(s, c).wait_send()
            hop_c(s, c).wait_send()
    xo_ref[...] = xs[2 * layers - 1]


def run_step(x_in, seq_lens, g_attn, g_mlp, w_q, b_q, w_k, b_k, w_v, b_v, w_o, w_gate, w_up, w_down, k_cache, v_cache):
    layers, batch, slots, kv, head = k_cache.shape
    width = x_in.shape[1]
    heads = w_q.shape[2] // head
    chunk = batch // 2
    flat = (layers, batch, slots * kv, head)
    exponent = -2.0 * (np.arange(head) % (head // 2)) / head
    freq = jnp.asarray((ROPE_THETA ** exponent)[None, :], F32)
    insts = 2 * layers * 2
    vmem = pl.BlockSpec(memory_space=pltpu.VMEM)
    hbm = pl.BlockSpec(memory_space=pl.ANY)
    weights = (w_q, w_k, w_v, w_o, w_gate, w_up, w_down)
    scratch = [pltpu.VMEM(w.shape, BF16) for w in weights]
    scratch += [
        pltpu.VMEM((chunk * 16, kv * chunk), BF16),
        pltpu.VMEM((chunk * heads, chunk * heads), BF16),
        pltpu.VMEM((chunk * heads, chunk * heads), BF16),
        pltpu.VMEM((chunk * 16, head), BF16),
        pltpu.VMEM((chunk * 16, head), BF16),
        pltpu.VMEM((chunk * heads, 2 * head), F32),
        pltpu.VMEM((chunk * heads, slots * kv), F32),
        pltpu.VMEM((chunk * heads, head), F32),
        pltpu.VMEM((batch * heads, slots * kv), F32),
        pltpu.VMEM((batch * 16, head), BF16),
        pltpu.VMEM((batch, head), F32),
        pltpu.VMEM((batch, head), F32),
        pltpu.VMEM((insts, chunk, width), BF16),
        pltpu.VMEM((insts, chunk // 2, width), BF16),
        pltpu.VMEM((insts, chunk // 2, width), BF16),
        pltpu.VMEM((insts, chunk // 2, width), BF16),
        pltpu.VMEM((2 * layers, batch, width), BF16),
        pltpu.SemaphoreType.DMA((layers, len(weights))),
        pltpu.SemaphoreType.DMA((layers, batch // BLK)),
        pltpu.SemaphoreType.DMA((layers, batch // BLK)),
        pltpu.SemaphoreType.DMA((3, insts)),
        pltpu.SemaphoreType.DMA((3, insts)),
    ]
    x_out, k_out, v_out = pl.pallas_call(
        functools.partial(step_kernel, chunk),
        out_shape=(jax.ShapeDtypeStruct(x_in.shape, BF16), pltpu.VMEM(flat, BF16), pltpu.VMEM(flat, BF16)),
        in_specs=[vmem] * 8 + [hbm] * 9,
        out_specs=(vmem, vmem, vmem),
        scratch_shapes=scratch,
        compiler_params=pltpu.CompilerParams(collective_id=0, has_side_effects=True, vmem_limit_bytes=28 * 2 ** 20),
        name="decode_step",
    )(x_in, seq_lens.reshape(1, batch), freq, g_attn, g_mlp, b_q, b_k, b_v, *weights, k_cache.reshape(flat), v_cache.reshape(flat))
    return x_out, k_out.reshape(k_cache.shape), v_out.reshape(v_cache.shape)


def solution(mesh):
    weight_col = P(None, None, "tp")
    weight_row = P(None, "tp", None)
    bias_col = P(None, "tp")
    cache_spec = P(None, "dp", None, "tp", None)
    in_specs = (P("dp", None), P("dp"), P(None, None), P(None, None), weight_col, bias_col, weight_col, bias_col, weight_col, bias_col, weight_row, weight_col, weight_col, weight_row, cache_spec, cache_spec)
    out_specs = (P("dp", None), cache_spec, cache_spec)
    return jax.shard_map(run_step, mesh=mesh, in_specs=in_specs, out_specs=out_specs, check_vma=False)
```

time: 286 us -> 65 us (0.23)
  other arithmetic: 160 us -> 0 us
  waiting for transfers between devices: 59.8 us -> 0 us
  Pallas kernels: 0 us -> 51.2 us
  matrix products: 50.3 us -> 0 us
  between operations: 14.1 us -> 0.65 us
  local copies, waits for them, and re-layouts: 0.86 us -> 13 us
    select_n x3 -> x0, other arithmetic: 93.3 us -> none  [the longest x2 51.8 us: attention(): k_next = jnp.where(is_new, k_rot[:, None], k_cache)]
    psum x4 -> x0, waiting for transfers between devices: 59.7 us -> none  [the longest x2 31.3 us: local_step(): x_cur = add_residual(x_cur, lax.psum(attn_part, 'tp'))]
    another operation x1 -> x0, other arithmetic: 52.9 us -> none  [local_step(): return (x_cur, jnp.stack(k_list), jnp.stack(v_list))]
    pallas_call x0 -> x1, Pallas kernels: none -> 51.2 us  [run_step(): pl.pallas_call(functools.partial(step_kernel, chunk), out_shape=(jax.Shap...]
    dot_general x14 -> x0, matrix products: 34.1 us -> none  [the longest x2 11.5 us: attention(): jnp.einsum('bkgs,bskd->bkgd', attn_probs, v_next, preferred_element_type=...]
    sub x2 -> x0, matrix products: 16.2 us -> none  [attention(): attn_probs = jax.nn.softmax(scores, axis=-1).astype(jnp.bfloat16)]
    unnamed x8 -> x5, local copies, waits for them, and re-layouts: 0.02 us -> 13 us
    reduce_sum x4 -> x0, other arithmetic: 4.49 us -> none  [rms_norm(): mean_sq = jnp.mean(vec_f32 * vec_f32, axis=-1, keepdims=True)]
  transfers between devices with their start and end apart: 4 -> 0, of which waited for: 2 -> 0; matrix products, arithmetic and copies ran while one was open for 33% -> 0% of each run, Pallas kernels for 0% -> 0%
where the time goes in v1:
time: 65 us; the launch traced here: 64.9 us
  Pallas kernels  51.2 us (79%)
  local copies, waits for them, and re-layouts  13 us (20%)
  between operations  0.65 us (1%)
    pallas_call x1, Pallas kernels, run_step(): pl.pallas_call(functools.partial(step_kernel, chunk), out_shape=(jax.Shap...  51.2 us
    unnamed x5, local copies, waits for them, and re-layouts  13 us

profile of v1, /device:TPU:0, one launch (start us, length us, event | category | flops | bytes accessed | tf_op | source)
XLA Modules:
  0.0 64.9 jit_solution(49147441972418373)
XLA Ops:
  0.6 51.2 %decode_step.1 = (bf16[128,1024]{1,0:T(8,128)(2,1)}, bf16[2,128,256,128]{3,2,1,0:T(8,128)(2,1)S(1)}, bf16[2,128,256,128]{3,2,1,0:T(8,128)(2,1)S(1)}) custom-call(bf16[128,1024]{1,0:T(8,128)(2,1)} %x_ref.1, s32[1,128]{1,0:T(1,128)} %bitcast.9, f32[1,128]{1,0:T(1,128)} %constant.2.clone.freq_ref, bf16[2,1024]{1,0:T(2,128)(2,1)} %g_attn_ref.1, ...), custom_call_target="tpu_custom_call" | custom-call | tf_op jit(solution)/shard_map/decode_step/pallas_call | solution.py:339
  51.8 6.2 %copy.23 = bf16[2,128,128,2,128]{4,3,2,1,0:T(2,128)(2,1)} copy(bf16[2,128,128,2,128]{4,3,2,1,0:T(2,128)(2,1)S(1)} %bitcast.6) | data formatting | bytes 33554432
  58.0 0.0 copy-start
  58.0 6.2 %copy.24 = bf16[2,128,128,2,128]{4,3,2,1,0:T(2,128)(2,1)} copy(bf16[2,128,128,2,128]{4,3,2,1,0:T(2,128)(2,1)S(1)} %bitcast.5) | data formatting | bytes 33554432
  64.1 0.0 copy-done
  64.2 0.7 %copy.25 = bf16[128,1024]{1,0:T(8,128)(2,1)} copy(bf16[128,1024]{1,0:T(8,128)(2,1)S(1)} %copy-done) | data formatting | bytes 524288
Async XLA Ops:
  58.0 6.2 %copy-start = (bf16[128,1024]{1,0:T(8,128)(2,1)S(1)}, bf16[128,1024]{1,0:T(8,128)(2,1)}, u32[]{:S(2)}) copy-start(bf16[128,1024]{1,0:T(8,128)(2,1)} %get-tuple-element.15) | copy-start | bytes 786436

commit v2 on v1

v2 whole, which is shorter than its diff:
```python
import functools

import jax
import jax.numpy as jnp
import numpy as np
from jax import lax
from jax.experimental import pallas as pl
from jax.experimental.pallas import tpu as pltpu
from jax.sharding import PartitionSpec as P

ROPE_THETA = 1000000.0
EPS = 1e-6
F32 = jnp.float32
BF16 = jnp.bfloat16
MESH = pl.DeviceIdType.MESH
BLK = 16
STEP = 32


def dot(lhs, rhs):
    return jnp.dot(lhs, rhs, preferred_element_type=F32)


def dot_nt(lhs, rhs):
    return lax.dot_general(lhs, rhs, (((1,), (1,)), ((), ())), preferred_element_type=F32)


def one_hot(shape, hit):
    rows = lax.broadcasted_iota(jnp.int32, shape, 0)
    cols = lax.broadcasted_iota(jnp.int32, shape, 1)
    return jnp.where(hit(rows, cols), 1.0, 0.0).astype(BF16)


def step_kernel(chunk, x_in, lens_in, freq_in, g_attn_in, g_mlp_in, bq_in, bk_in, bv_in,
                wq_hbm, wk_hbm, wv_hbm, wo_hbm, wg_hbm, wu_hbm, wd_hbm, kc_hbm, vc_hbm,
                xo_ref, sum_ref, kn_ref, vn_ref, kv_out,
                x_ref, lens_ref, freq_ref, g_attn_ref, g_mlp_ref, bq_ref, bk_ref, bv_ref,
                wq, wk, wv, wo, wg, wu, wd,
                gather, ungather, gather_kv, pairs, qlhs, scores, fresh, rows_out, limit, cos_t, sin_t,
                part, recv_a, mid, recv_b, recv_d, xs,
                s_sem, w_sem, k_sem, v_sem, send_sem, recv_sem):
    ko_ref, vo_ref = kv_out.at[0], kv_out.at[1]
    layers, batch, slots2, head = kv_out.shape[1:]
    heads = wq.shape[2] // head
    kv = wk.shape[2] // head
    group = heads // kv
    n_chunks = batch // chunk
    half = chunk // 2
    blocks = chunk // BLK
    tp = lax.axis_index("tp")
    core = lax.rem(tp, 2)
    chip = tp // 2
    core_peer = {"tp": chip * 2 + (1 - core)}
    chip_peer = {"tp": (1 - chip) * 2 + core}

    weights = ((wq_hbm, wq), (wk_hbm, wk), (wv_hbm, wv), (wo_hbm, wo), (wg_hbm, wg), (wu_hbm, wu), (wd_hbm, wd))

    def weight_copy(layer, idx):
        src, dst = weights[idx]
        return pltpu.make_async_copy(src.at[layer], dst.at[layer], w_sem.at[layer, idx])

    def cache_copy(src, dst, sem, layer, blk):
        return pltpu.make_async_copy(src.at[layer, pl.ds(blk * BLK, BLK)], dst.at[layer, pl.ds(blk * BLK, BLK)], sem.at[layer, blk])

    def start_weights(layer, idxs):
        for idx in idxs:
            weight_copy(layer, idx).start()

    def wait_weights(layer, idxs):
        for idx in idxs:
            weight_copy(layer, idx).wait()

    def start_cache(layer, c):
        for src, dst, sem in ((kc_hbm, ko_ref, k_sem), (vc_hbm, vo_ref, v_sem)):
            @pl.loop(0, blocks)
            def _(i):
                cache_copy(src, dst, sem, layer, c * blocks + i).start()

    smalls = ((x_in, x_ref), (lens_in, lens_ref), (freq_in, freq_ref), (g_attn_in, g_attn_ref), (g_mlp_in, g_mlp_ref),
              (bq_in, bq_ref), (bk_in, bk_ref), (bv_in, bv_ref))
    for i, (src, dst) in enumerate(smalls):
        pltpu.make_async_copy(src, dst, s_sem.at[i]).start()
    start_weights(0, (0, 1, 2))
    start_cache(0, 0)

    barrier = pltpu.get_barrier_semaphore()
    for peer in (core_peer, chip_peer):
        pl.semaphore_signal(barrier, inc=1, device_id=peer, device_id_type=MESH)

    gather[...] = one_hot(gather.shape, lambda r, c: c == (r % heads) * chunk + r // heads)
    ungather[...] = one_hot(ungather.shape, lambda r, c: r == (c % heads) * chunk + c // heads)
    gather_kv[...] = one_hot(gather_kv.shape, lambda r, c: c == (r % heads) // group * chunk + r // heads)
    pairs[...] = one_hot(pairs.shape, lambda r, c: c == (r % kv) * chunk + r // kv)
    for i, (src, dst) in enumerate(smalls):
        pltpu.make_async_copy(src, dst, s_sem.at[i]).wait()
    lens = lens_ref[...].astype(F32)
    sq = (batch, batch)
    diag = lax.broadcasted_iota(jnp.int32, sq, 0) == lax.broadcasted_iota(jnp.int32, sq, 1)
    len_col = jnp.sum(jnp.where(diag, jnp.broadcast_to(lens, sq), 0.0), axis=1, keepdims=True)
    len_cols = jnp.broadcast_to(len_col, (batch, head))
    angles = len_cols * freq_ref[...]
    cos_t[...] = jnp.cos(angles)
    lane = lax.broadcasted_iota(jnp.int32, (batch, head), 1)
    sine = jnp.sin(angles)
    sin_t[...] = jnp.where(lane < head // 2, -sine, sine)
    len_bf = len_cols.astype(BF16)
    row_len = dot(one_hot((batch * heads, batch), lambda r, c: c == r // heads), len_bf)
    row_len = jnp.concatenate([row_len] * (slots2 // head), axis=1)
    lim_shape = (batch * heads, slots2)
    q_head = lax.broadcasted_iota(jnp.int32, lim_shape, 0) % heads
    own = lax.broadcasted_iota(jnp.int32, lim_shape, 1) % kv == q_head // group
    limit[...] = jnp.where(own, row_len, -1.0)

    def rms_norm(x_bf, gain_ref, layer):
        x = x_bf.astype(F32)
        mean_sq = jnp.mean(x * x, axis=-1, keepdims=True)
        return (x * lax.rsqrt(mean_sq + EPS) * gain_ref[pl.ds(layer, 1), :].astype(F32)).astype(BF16)

    def read_x(stage, c):
        src = x_ref if stage == 0 else xs.at[stage - 1]
        return src[pl.ds(c * chunk, chunk), :]

    def qkv(layer, c):
        h = rms_norm(read_x(2 * layer, c), g_attn_ref, layer)
        cos = cos_t[pl.ds(c * chunk, chunk), :]
        sin = sin_t[pl.ds(c * chunk, chunk), :]

        def rope(vec):
            return (vec * cos + pltpu.roll(vec, head // 2, 1) * sin).astype(BF16)

        def split(mat, n):
            return [mat[:, i * head:(i + 1) * head] for i in range(n)]

        q = dot(h, wq[layer]) + bq_ref[pl.ds(layer, 1), :].astype(F32)
        k = dot(h, wk[layer]) + bk_ref[pl.ds(layer, 1), :].astype(F32)
        v = dot(h, wv[layer]) + bv_ref[pl.ds(layer, 1), :].astype(F32)
        q_stack = jnp.concatenate([rope(m) for m in split(q, heads)], axis=0)
        k_stack = jnp.concatenate([rope(m) for m in split(k, kv)], axis=0)
        v_stack = jnp.concatenate([m.astype(BF16) for m in split(v, kv)], axis=0)
        kn_ref[layer, pl.ds(c * kv * chunk, kv * chunk), :] = dot(pairs[...], k_stack).astype(BF16)
        vn_ref[layer, pl.ds(c * kv * chunk, kv * chunk), :] = dot(pairs[...], v_stack).astype(BF16)
        q_rows = dot(gather[...], q_stack)
        k_rows = dot(gather_kv[...], k_stack)
        fresh[...] = dot(gather_kv[...], v_stack)
        first = lax.broadcasted_iota(jnp.int32, q_rows.shape, 0) % (2 * heads) < heads
        qlhs[...] = jnp.concatenate([jnp.where(first, q_rows, 0.0), jnp.where(first, 0.0, q_rows)], axis=1)
        return jnp.sum(q_rows * k_rows, axis=-1, keepdims=True)

    def by_pairs(src, dst, sem, layer, c, one_pair):
        @pl.loop(0, chunk // STEP)
        def _(i):
            for j in range(STEP // BLK):
                cache_copy(src, dst, sem, layer, c * blocks + i * (STEP // BLK) + j).wait()
            for pair in range(STEP // 2):
                b = i * STEP + 2 * pair
                row = c * chunk + b
                rhs = jnp.concatenate([dst[layer, row], dst[layer, row + 1]], axis=1)
                one_pair(pl.ds(pl.multiple_of(b * heads, 2 * heads), 2 * heads), rhs)

    def attn_scores(layer, c):
        def one_pair(rows, rhs):
            scores[rows, :] = dot_nt(qlhs[rows, :].astype(BF16), rhs)

        by_pairs(kc_hbm, ko_ref, k_sem, layer, c, one_pair)

    def attn_softmax(c, new_score):
        s = scores[...] * (head ** -0.5)
        s_new = new_score * (head ** -0.5)
        slot = (lax.broadcasted_iota(jnp.int32, s.shape, 1) // kv).astype(F32)
        s = jnp.where(slot < limit[pl.ds(c * chunk * heads, chunk * heads), :], s, -1e30)
        top = jnp.maximum(jnp.max(s, axis=-1, keepdims=True), s_new)
        e = jnp.exp(s - top)
        e_new = jnp.exp(s_new - top)
        total = jnp.sum(e, axis=-1, keepdims=True) + e_new
        scores[...] = e / total
        fresh[...] = fresh[...] * (e_new / total).astype(BF16).astype(F32)

    def attn_values(layer, c):
        def one_pair(rows, rhs):
            out = dot(scores[rows, :].astype(BF16), rhs)
            first = lax.broadcasted_iota(jnp.int32, (2 * heads, head), 0) < heads
            rows_out[rows, :] = jnp.where(first, out[:, :head], out[:, head:]) + fresh[rows, :]

        by_pairs(vc_hbm, vo_ref, v_sem, layer, c, one_pair)

    def attn_project(layer, c):
        stacked = dot(ungather[...], rows_out[...].astype(BF16)).astype(BF16)
        attn = jnp.concatenate([stacked[i * chunk:(i + 1) * chunk, :] for i in range(heads)], axis=1)
        part[2 * layer * n_chunks + c] = dot(attn, wo[layer]).astype(BF16)

    def mlp(layer, c):
        h = rms_norm(read_x(2 * layer + 1, c), g_mlp_ref, layer)
        act = (jax.nn.silu(dot(h, wg[layer])) * dot(h, wu[layer])).astype(BF16)
        part[(2 * layer + 1) * n_chunks + c] = dot(act, wd[layer]).astype(BF16)

    last = 2 * layers - 1
    mine = pl.ds(pl.multiple_of(core * half, half), half)
    other = pl.ds(pl.multiple_of((1 - core) * half, half), half)

    def send(hop, inst, src, dst, peer):
        return pltpu.make_async_remote_copy(src_ref=src, dst_ref=dst, send_sem=send_sem.at[hop, inst], recv_sem=recv_sem.at[hop, inst],
                                            device_id=peer, device_id_type=MESH)

    def hop_a(s, c):
        inst = s * n_chunks + c
        return send(0, inst, part.at[inst, other], recv_a.at[inst], core_peer)

    def hop_b(s, c):
        inst = s * n_chunks + c
        return send(1, inst, mid.at[inst], recv_b.at[inst], chip_peer)

    def hop_c(s, c):
        rows = pl.ds(pl.multiple_of(c * chunk + core * half, half), half)
        return send(2, s * n_chunks + c, xs.at[s, rows], xs.at[s, rows], core_peer)

    def hop_d(s, c):
        inst = s * n_chunks + c
        return send(3, inst, part.at[inst], recv_d.at[c], core_peer)

    def sum_start(s, c):
        (hop_d if s == last else hop_a)(s, c).start()

    def chip_sum(c):
        inst = last * n_chunks + c
        hop_d(last, c).wait_recv()
        sum_ref[pl.ds(c * chunk, chunk), :] = (part[inst].astype(F32) + recv_d[c].astype(F32)).astype(BF16)

    def sum_cross(s, c):
        inst = s * n_chunks + c
        hop_a(s, c).wait_recv()
        mid[inst] = (part[inst, mine, :].astype(F32) + recv_a[inst].astype(F32)).astype(BF16)
        hop_b(s, c).start()

    def sum_share(s, c):
        inst = s * n_chunks + c
        hop_b(s, c).wait_recv()
        rows = pl.ds(pl.multiple_of(c * chunk + core * half, half), half)
        before = (x_ref if s == 0 else xs.at[s - 1])[rows, :]
        total = mid[inst].astype(F32) + recv_b[inst].astype(F32)
        xs[s, rows, :] = (before.astype(F32) + total).astype(BF16)
        hop_c(s, c).start()

    def sum_end(s, c):
        hop_c(s, c).wait_recv()

    def flow(layer):
        s = 2 * layer
        wait_weights(layer, (0, 1, 2))
        if layer == 0:
            start_weights(0, (3,))
            start_cache(0, 1)
        else:
            sum_end(s - 1, 0)
        new_score = qkv(layer, 0)
        attn_scores(layer, 0)
        if layer > 0:
            sum_share(s - 1, 1)
        attn_softmax(0, new_score)
        attn_values(layer, 0)
        wait_weights(layer, (3,))
        attn_project(layer, 0)
        if layer == 0:
            pl.semaphore_wait(barrier, 2)
        sum_start(s, 0)
        if layer == 0:
            start_weights(0, (4, 5, 6))
            start_weights(1, (0, 1, 2))
            start_cache(1, 0)
        else:
            sum_end(s - 1, 1)
        new_score = qkv(layer, 1)
        sum_cross(s, 0)
        attn_scores(layer, 1)
        attn_softmax(1, new_score)
        attn_values(layer, 1)
        attn_project(layer, 1)
        sum_start(s, 1)
        if layer == 0:
            start_cache(1, 1)
            start_weights(1, (3, 4, 5, 6))
        sum_share(s, 0)
        sum_cross(s, 1)
        wait_weights(layer, (4, 5, 6))
        sum_end(s, 0)
        mlp(layer, 0)
        sum_start(s + 1, 0)
        sum_share(s, 1)
        if s + 1 < last:
            sum_cross(s + 1, 0)
        sum_end(s, 1)
        mlp(layer, 1)
        sum_start(s + 1, 1)
        if s + 1 < last:
            sum_cross(s + 1, 1)
            sum_share(s + 1, 0)
        else:
            chip_sum(0)
            xo_ref[...] = xs[last - 1]
            chip_sum(1)

    for layer in range(layers):
        flow(layer)
    for s in range(last + 1):
        for c in range(n_chunks):
            for hop in (hop_d,) if s == last else (hop_a, hop_b, hop_c):
                hop(s, c).wait_send()


def write_kernel(lens_ref, kv_ref, kn_ref, vn_ref, ko_hbm, vo_hbm, sem, row_sem):
    k_ref, v_ref = kv_ref.at[0], kv_ref.at[1]
    layers, batch = kv_ref.shape[1:3]
    sides = ((k_ref, kn_ref, ko_hbm), (v_ref, vn_ref, vo_hbm))
    blocks = batch // BLK

    def copy(side, layer, blk):
        src, _, dst = sides[side]
        rows = pl.ds(blk * BLK, BLK)
        return pltpu.make_async_copy(src.at[layer, rows], dst.at[layer, rows], sem.at[side, layer, blk])

    for layer in range(layers):
        for side in range(2):
            @pl.loop(0, blocks)
            def _(blk):
                copy(side, layer, blk).start()

    for layer in range(layers):
        for side in range(2):
            _, new, dst = sides[side]

            @pl.loop(0, blocks)
            def _(blk):
                copy(side, layer, blk).wait()
                for i in range(BLK):
                    b = blk * BLK + i
                    pltpu.make_async_copy(new.at[layer, b], dst.at[layer, b, lens_ref[b]], row_sem.at[side]).start()

    for side in range(2):
        _, new, dst = sides[side]
        pltpu.make_async_copy(new, dst.at[:, :, 0], row_sem.at[side]).wait()


def run_step(x_in, seq_lens, g_attn, g_mlp, w_q, b_q, w_k, b_k, w_v, b_v, w_o, w_gate, w_up, w_down, k_cache, v_cache):
    layers, batch, slots, kv, head = k_cache.shape
    width = x_in.shape[1]
    heads = w_q.shape[2] // head
    chunk = batch // 2
    flat = (layers, batch, slots * kv, head)
    exponent = -2.0 * (np.arange(head) % (head // 2)) / head
    freq = jnp.asarray((ROPE_THETA ** exponent)[None, :], F32)
    insts = 2 * layers * 2
    vmem = pl.BlockSpec(memory_space=pltpu.VMEM)
    hbm = pl.BlockSpec(memory_space=pl.ANY)
    smalls = (x_in, seq_lens.reshape(1, batch), freq, g_attn, g_mlp, b_q, b_k, b_v)
    weights = (w_q, w_k, w_v, w_o, w_gate, w_up, w_down)
    rows = chunk * heads
    half = chunk // 2
    scratch = [pltpu.VMEM(a.shape, a.dtype) for a in smalls + weights]
    scratch += [
        pltpu.VMEM((rows, rows), BF16),
        pltpu.VMEM((rows, rows), BF16),
        pltpu.VMEM((rows, kv * chunk), BF16),
        pltpu.VMEM((kv * chunk, kv * chunk), BF16),
        pltpu.VMEM((rows, 2 * head), F32),
        pltpu.VMEM((rows, slots * kv), F32),
        pltpu.VMEM((rows, head), F32),
        pltpu.VMEM((rows, head), F32),
        pltpu.VMEM((batch * heads, slots * kv), F32),
        pltpu.VMEM((batch, head), F32),
        pltpu.VMEM((batch, head), F32),
        pltpu.VMEM((insts, chunk, width), BF16),
        pltpu.VMEM((insts, half, width), BF16),
        pltpu.VMEM((insts, half, width), BF16),
        pltpu.VMEM((insts, half, width), BF16),
        pltpu.VMEM((2, chunk, width), BF16),
        pltpu.VMEM((2 * layers - 1, batch, width), BF16),
        pltpu.SemaphoreType.DMA((len(smalls),)),
        pltpu.SemaphoreType.DMA((layers, len(weights))),
        pltpu.SemaphoreType.DMA((layers, batch // BLK)),
        pltpu.SemaphoreType.DMA((layers, batch // BLK)),
        pltpu.SemaphoreType.DMA((4, insts)),
        pltpu.SemaphoreType.DMA((4, insts)),
    ]
    fresh = pltpu.VMEM((layers, batch * kv, head), BF16)
    x_mid, share, k_new, v_new, held_kv = pl.pallas_call(
        functools.partial(step_kernel, chunk),
        out_shape=(pltpu.VMEM(x_in.shape, BF16), pltpu.VMEM(x_in.shape, BF16), fresh, fresh, pltpu.VMEM((2,) + flat, BF16)),
        in_specs=[hbm] * 17,
        out_specs=(vmem,) * 5,
        scratch_shapes=scratch,
        compiler_params=pltpu.CompilerParams(collective_id=0, has_side_effects=True, vmem_limit_bytes=26 * 2 ** 20),
        cost_estimate=pl.CostEstimate(flops=2 * 10 ** 10, bytes_accessed=5 * 10 ** 7, transcendentals=0),
        name="decode_step",
    )(*smalls, *weights, k_cache.reshape(flat), v_cache.reshape(flat))

    ranks = lax.axis_size("tp")
    other_share = lax.ppermute(share, "tp", [(i, (i + ranks // 2) % ranks) for i in range(ranks)])
    new_rows = (layers, batch, kv, head)
    held = (held_kv.reshape((2,) + k_cache.shape), k_new.reshape(new_rows), v_new.reshape(new_rows))
    cache_out = jax.ShapeDtypeStruct(k_cache.shape, BF16)
    k_out, v_out = pl.pallas_call(
        write_kernel,
        out_shape=(cache_out, cache_out),
        in_specs=[pl.BlockSpec(memory_space=pltpu.SMEM)] + [vmem] * 3,
        out_specs=(hbm, hbm),
        scratch_shapes=[pltpu.SemaphoreType.DMA((2, layers, batch // BLK)), pltpu.SemaphoreType.DMA((2,))],
        compiler_params=pltpu.CompilerParams(vmem_limit_bytes=2 ** 20),
        cost_estimate=pl.CostEstimate(flops=2 * 10 ** 10, bytes_accessed=4 * 10 ** 7, transcendentals=0),
        name="write_caches",
    )(seq_lens, *held)
    x_out = (x_mid.astype(F32) + (share.astype(F32) + other_share.astype(F32))).astype(BF16)
    return x_out, k_out, v_out


def solution(mesh):
    weight_col = P(None, None, "tp")
    weight_row = P(None, "tp", None)
    bias_col = P(None, "tp")
    cache_spec = P(None, "dp", None, "tp", None)
    in_specs = (P("dp", None), P("dp"), P(None, None), P(None, None), weight_col, bias_col, weight_col, bias_col, weight_col, bias_col, weight_row, weight_col, weight_col, weight_row, cache_spec, cache_spec)
    out_specs = (P("dp", None), cache_spec, cache_spec)
    return jax.shard_map(run_step, mesh=mesh, in_specs=in_specs, out_specs=out_specs, check_vma=False)
```

time: 65 us -> 52.7 us (0.81)
  local copies, waits for them, and re-layouts: 13 us -> 0.01 us
  Pallas kernels: 51.2 us -> 50.2 us
  other arithmetic: 0 us -> 0.83 us
  starting transfers between devices: 0 us -> 0.83 us
    unnamed x5 -> x2, local copies, waits for them, and re-layouts: 13 us -> 0.01 us
    pallas_call x1 -> x2, Pallas kernels: 51.2 us -> 50.2 us  [the longest x1 36.8 us: run_step(): pl.pallas_call(functools.partial(step_kernel, chunk), out_shape=(pltpu.VM...]
    ppermute x0 -> x1, starting transfers between devices: none -> 0.83 us  [run_step(): lax.ppermute(share, 'tp', [(i, (i + ranks // 2) % ranks) for i in range(r...]
    convert_element_type x0 -> x1, other arithmetic: none -> 0.83 us  [run_step(): (x_mid.astype(F32) + (share.astype(F32) + other_share.astype(F32))).astyp...]
  transfers between devices with their start and end apart: 0 -> 1, of which waited for: 0 -> 0; matrix products, arithmetic and copies ran while one was open for 0% -> 0% of each run, Pallas kernels for 0% -> 26%
where the time goes in v2:
time: 52.7 us; the launch traced here: 52.6 us
  Pallas kernels  50.2 us (95%)
  starting transfers between devices  0.83 us (2%)
  other arithmetic  0.83 us (2%)
  between operations  0.67 us (1%)
    pallas_call x1, Pallas kernels, run_step(): pl.pallas_call(functools.partial(step_kernel, chunk), out_shape=(pltpu.VM...  36.8 us
    pallas_call x1, Pallas kernels, run_step(): pl.pallas_call(write_kernel, out_shape=(cache_out, cache_out), in_specs=[...  13.4 us
  transfers between devices with their start and end apart: 1, of which 0 were waited for; matrix products, arithmetic and copies ran while one was open for 0% of the time, Pallas kernels for 26%

profile of v2, /device:TPU:0, one launch (start us, length us, event | category | flops | bytes accessed | tf_op | source)
XLA Modules:
  0.0 52.6 jit_solution(18432140463025237783)
XLA Ops:
  0.6 0.0 copy-start
  0.6 36.8 %decode_step.1 = (bf16[128,1024]{1,0:T(8,128)(2,1)S(1)}, bf16[128,1024]{1,0:T(8,128)(2,1)S(1)}, bf16[2,256,128]{2,1,0:T(8,128)(2,1)S(1)}, bf16[2,256,128]{2,1,0:...) custom-call(bf16[128,1024]{1,0:T(8,128)(2,1)} %x_in.1, s32[1,128]{1,0:T(1,128)} %bitcast.6, f32[1,128]{1,0:T(1,128)} %constant.2.clone.freq_in, ...), custom_call_target="tpu_custom_call" | custom-call | flops 20000000000 | bytes 50000000 | tf_op jit(solution)/shard_map/decode_step/pallas_call | solution.py:384
  37.5 0.8 %collective-permute-start = (bf16[128,1024]{1,0:T(8,128)(2,1)S(1)}, bf16[128,1024]{1,0:T(8,128)(2,1)S(1)}, u32[]{:S(2)}, u32[]{:S(2)}) collective-permute-start(bf16[128,1024]{1,0:T(8,128)(2,1)S(1)} %get-tuple-element.11), channel_id=1, source_target_pairs={{0,2},{1,3},{2,0},{3,1},{4,6},{5,7},{6,4},{7,5},{8,10},{9,11},{10,... | collective-permute-start | bytes 786440 | tf_op jit(solution)/shard_map/ppermute | solution.py:396
  38.3 0.0 copy-done
  38.3 13.4 %write_caches.1 = (bf16[2,128,128,2,128]{4,3,2,1,0:T(2,128)(2,1)}, bf16[2,128,128,2,128]{4,3,2,1,0:T(2,128)(2,1)}) custom-call(s32[128]{0:T(128)S(1)} %copy-done, bf16[2,2,128,128,2,128]{5,4,3,2,1,0:T(2,128)(2,1)S(1)} %bitcast.7, bf16[2,128,2,128]{3,2,1,0:T(2,128)(2,1)S(1)} %bitcast.8, bf16[2,128,2,128]{3,2,1,0:T(2,128)(2,1)S(1)} %bitcast.9), custom_call_target="tpu_custom_call" | custom-call | flops 20000000000 | bytes 40000000 | tf_op jit(solution)/shard_map/write_caches/pallas_call | solution.py:400
  51.7 0.0 collective-permute-done
  51.7 0.8 %add_convert_fusion = bf16[128,1024]{1,0:T(8,128)(2,1)} fusion(bf16[128,1024]{1,0:T(8,128)(2,1)S(1)} %collective-permute-done, bf16[128,1024]{1,0:T(8,128)(2,1)S(1)} %get-tuple-element.11, bf16[128,1024]{1,0:T(8,128)(2,1)S(1)} %get-tuple-element.10), kind=kLoop, calls=%fused_computation | loop fusion | flops 786432 | bytes 1048576 | tf_op jit(solution)/shard_map/convert_element_type | solution.py:410
Async XLA Ops:
  0.6 37.6 %copy-start = (s32[128]{0:T(128)S(1)}, s32[128]{0:T(128)}, u32[]{:S(2)}) copy-start(s32[128]{0:T(128)} %lens_ref.1) | copy-start | bytes 1540
  37.5 14.3 %collective-permute-start = (bf16[128,1024]{1,0:T(8,128)(2,1)S(1)}, bf16[128,1024]{1,0:T(8,128)(2,1)S(1)}, u32[]{:S(2)}, u32[]{:S(2)}) collective-permute-start(bf16[128,1024]{1,0:T(8,128)(2,1)S(1)} %get-tuple-element.11), channel_id=1, source_target_pairs={{0,2},{1,3},{2,0},{3,1},{4,6},{5,7},{6,4},{7,5},{8,10},{9,11},{10,... | collective-permute-start | bytes 786440 | tf_op jit(solution)/shard_map/ppermute | solution.py:396
